TPU v7x, 512 devices: a whole 4x8x8 slice. The times are simulated.
512 devices in a mesh: paths: 16 (over y, core), contract: 32 (over z, x).
Axes of the slice: x: 4, y: 8, z: 8, core: 2. Of those that a mesh axis runs over, the one named last changes fastest.
Arguments:
- prices: float32 [1, 2048], P(None, 'paths'), may hold values from -6 to 6
- terminal: bfloat16 [2048, 2048, 128], P('contract', 'paths'), may hold values from -6 to 6
- band: int32 [2048], replicated, may hold values from 32 to 128
- position: int32 [2048], replicated, may hold values from 0 to 2047, as said below
- actions: int32 [2048, 3], replicated, may hold values from -3 to 3
- degree: int32 [2048], replicated, may hold values from 2 to 7
- volume: float32 [2048], replicated, may hold values from 0.05 to 0.5
Outputs:
- valued: bfloat16 [2048, 2048, 128], P('contract', 'paths')
Inputs may be any that keep to these rules, and one draw needn't show every extreme that they name: A permutation of the contracts; contract c goes to new block position[c] // 64. Each old block of 64 contracts sends exactly 2 contracts to each of the 32 new blocks.
All inputs are finite; a program needn't handle non-finite values.
Results may differ from a plain program's by a relative error of at most 0.0038.
Values may be sent and summed in bfloat16 or wider, within the bound.
A program may use at most 64 MiB of HBM per device.

v0:
```python
import jax
import jax.numpy as jnp
from jax import lax
from jax.sharding import PartitionSpec as P

LEVELS = 128
BASIS = 8
MOVE = 3


RIDGE = 0.05
DISCOUNT = 0.98
SPOT_SCALE = 0.25


def in_blocks(shard, dim, size):
    dims = shard.shape
    pieces = shard.reshape(*dims[:dim], size, dims[dim] // size, *dims[dim + 1 :])
    return jnp.moveaxis(pieces, dim, 0)


def summed_on_arrival(shard, axis, dim):
    pieces = in_blocks(shard, dim, lax.axis_size(axis))
    arrived = lax.all_to_all(pieces, axis, split_axis=0, concat_axis=0, tiled=True)
    return arrived.astype(jnp.float32).sum(axis=0)


def sent_to_all(shard, axis):
    size = lax.axis_size(axis)
    return lax.all_to_all(
        jnp.broadcast_to(shard[None], (size, *shard.shape)), axis, 0, 0, tiled=True
    )


def taken_together(shard, axis):
    return sent_to_all(shard, axis).sum(axis=0)


def laid_out(pieces, dim):
    pieces = jnp.moveaxis(pieces, 0, dim)
    dims = pieces.shape
    return pieces.reshape(*dims[:dim], dims[dim] * dims[dim + 1], *dims[dim + 2 :])


def gather_directly(shard, axis, dim):
    pieces = sent_to_all(shard, axis)
    return laid_out(pieces, dim)


def chebyshev(prices_row):
    scaled = jnp.tanh(prices_row)
    series = [jnp.ones_like(scaled), scaled]
    for order in range(2, BASIS):
        series.append(2.0 * scaled * series[-1] - series[-2])
    return jnp.stack(series[:BASIS])


def regress(gram, moments, path_count, degree_block):
    orders = jnp.arange(BASIS, dtype=jnp.int32)
    keep_basis = (orders[None, :] <= degree_block[:, None]).astype(jnp.float32)
    identity = jnp.eye(BASIS, dtype=jnp.float32)
    system = keep_basis[:, :, None] * keep_basis[:, None, :] * (gram / path_count)[None]
    system = system + (1.0 - keep_basis)[:, :, None] * identity[None] + RIDGE * identity[None]
    scaled_moments = keep_basis[:, :, None] * (moments / path_count)
    factor = jnp.linalg.cholesky(system)
    halfway = lax.linalg.triangular_solve(factor, scaled_moments, left_side=True, lower=True)
    return lax.linalg.triangular_solve(
        factor, halfway, left_side=True, lower=True, transpose_a=True
    )


def decide(values_now, estimate, spot_price, band_block, action_block, volume_block):
    levels = jnp.arange(LEVELS, dtype=jnp.int32)
    living = levels[None, :] < band_block[:, None]
    padded = jnp.pad(estimate, ((0, 0), (0, 0), (MOVE, MOVE)))
    optimum = DISCOUNT * estimate
    for offset in range(-MOVE, MOVE + 1):
        if offset == 0:
            continue
        allowed = jnp.any(action_block == offset, axis=1)
        target_level = levels + offset
        inside = (target_level[None, :] >= 0) & (target_level[None, :] < band_block[:, None])
        moved = padded[:, :, MOVE + offset : MOVE + offset + LEVELS]
        candidate = (
            -offset * volume_block[:, None, None] * spot_price[None, :, None] + DISCOUNT * moved
        )
        usable = allowed[:, None, None] & inside[:, None, :]
        optimum = jnp.where(usable, jnp.maximum(optimum, candidate), optimum)
    return jnp.where(living[:, None, :], optimum + DISCOUNT * (values_now - estimate), 0.0)


def lookup_flat(contract_ids, table):
    matches = contract_ids[:, None] == jnp.arange(table.shape[0], dtype=jnp.int32)[None, :]
    return jnp.sum(jnp.where(matches, table[None, :], jnp.zeros((), table.dtype)), axis=1)


def lookup_rows(contract_ids, table):
    matches = contract_ids[:, None] == jnp.arange(table.shape[0], dtype=jnp.int32)[None, :]
    return jnp.sum(
        jnp.where(matches[:, :, None], table[None, :, :], jnp.zeros((), table.dtype)), axis=1
    )


def redistribute(grids, position, block_count, myself, capacity):
    con_count = grids.shape[0]
    slot_ids = jnp.arange(con_count, dtype=jnp.int32)
    target = position // con_count
    target_grid = target.reshape(block_count, con_count)
    mine = lax.dynamic_slice_in_dim(target, myself * con_count, con_count)
    earlier = slot_ids[None, :] < slot_ids[:, None]
    rank_out = jnp.sum(earlier & (mine[None, :] == mine[:, None]), axis=1)
    flat_slot = mine * capacity + rank_out
    send_slots = jnp.arange(block_count * capacity, dtype=jnp.int32)
    matches = flat_slot[None, :] == send_slots[:, None]
    source_row = jnp.sum(jnp.where(matches, slot_ids[None, :], 0), axis=1)
    filled = jnp.any(matches, axis=1)
    outgoing = jnp.where(filled[:, None, None], grids[source_row], jnp.zeros((), grids.dtype))
    outgoing = outgoing.reshape((block_count, capacity) + grids.shape[1:])
    incoming = lax.all_to_all(outgoing, "contract", split_axis=0, concat_axis=0, tiled=True)
    wanted = myself * con_count + slot_ids
    owner_match = position[None, :] == wanted[:, None]
    owner_ids = jnp.sum(
        jnp.where(owner_match, jnp.arange(position.shape[0], dtype=jnp.int32)[None, :], 0), axis=1
    )
    source_block = owner_ids // con_count
    source_slot = owner_ids % con_count
    block_match = source_block[:, None] == jnp.arange(block_count, dtype=jnp.int32)[None, :]
    peer_targets = jnp.sum(jnp.where(block_match[:, :, None], target_grid[None, :, :], 0), axis=1)
    rank_in = jnp.sum((slot_ids[None, :] < source_slot[:, None]) & (peer_targets == myself), axis=1)
    chosen = source_block * capacity + rank_in
    arrived = incoming.reshape((block_count * capacity,) + grids.shape[1:])[chosen]
    return (arrived, owner_ids)


def window(prices, values_now, contract_ids, band, actions, degree, volume, path_count):
    highest = lax.Precision.HIGHEST
    band_block = lookup_flat(contract_ids, band)
    degree_block = lookup_flat(contract_ids, degree)
    volume_block = lookup_flat(contract_ids, volume)
    action_block = lookup_rows(contract_ids, actions)
    basis_rows = chebyshev(prices[0])
    spot_price = jnp.exp(SPOT_SCALE * prices[0])
    gram_part = jnp.dot(basis_rows, basis_rows.T, precision=highest)
    moments = jnp.einsum("kp,cpl->ckl", basis_rows, values_now, precision=highest)
    moments_share = summed_on_arrival(moments.astype(jnp.bfloat16), "paths", 2)
    gram = taken_together(gram_part, "paths")
    fitted_share = regress(gram, moments_share, path_count, degree_block)
    fitted = gather_directly(fitted_share, "paths", 2)
    estimate = jnp.einsum("kp,ckl->cpl", basis_rows, fitted, precision=highest)
    values_now = decide(values_now, estimate, spot_price, band_block, action_block, volume_block)
    return values_now


def per_device(prices, terminal, band, position, actions, degree, volume):
    block_count = lax.axis_size("contract")
    myself = lax.axis_index("contract")
    con_count = terminal.shape[0]
    capacity = con_count // block_count
    path_count = prices.shape[1] * lax.axis_size("paths")
    grids, contract_ids = redistribute(terminal, position, block_count, myself, capacity)
    values_now = window(
        prices, grids.astype(jnp.float32), contract_ids, band, actions, degree, volume, path_count
    )
    result = values_now.astype(jnp.bfloat16)
    return result


def solution(mesh):
    in_specs = (P(None, "paths"), P("contract", "paths", None), P(), P(), P(), P(), P())
    out_specs = P("contract", "paths", None)
    return jax.shard_map(
        per_device, mesh=mesh, in_specs=in_specs, out_specs=out_specs, check_vma=False
    )
```

profile of v0, /device:TPU:1, one launch (start us, length us, event | category | flops | bytes accessed | tf_op | source)
XLA Modules:
  0.0 148.3 jit_solution(17491151203642367101)
XLA Ops:
  0.0 0.8 exponential_bitcast_fusion
  0.8 0.7 multiply_subtract_fusion.1
  1.6 0.6 broadcast_in_dim.172
  2.3 10.1 %all-to-all-start = ((f32[16,8,8]{2,1,0:T(8,128)}), f32[16,8,8]{2,1,0:T(8,128)S(1)}, u32[]{:S(2)}, u32[]{:S(2)}) async-start(f32[16,8,8]{2,1,0:T(8,128)} %broadcast_in_dim.172), calls=%async_computation | async-start | bytes 131072 | tf_op jit(solution)/shard_map/all_to_all | solution.py:30
  12.4 0.7 add_select_fusion
  13.7 0.9 select_reduce_fusion.5
  14.8 2.1 %gather_fusion = bf16[64,128,128]{2,1,0:T(8,128)(2,1)} fusion(bf16[64,128,128]{2,1,0:T(8,128)(2,1)S(1)} %copy-done, s32[1024]{0:T(1024)S(1)} %pad_clamp_fusion.1), kind=kCustom, calls=%fused_computation | custom fusion | bytes 4194560 | tf_op jit(solution)/shard_map/gather | solution.py:117
  16.9 3.1 %broadcast_select_fusion = bf16[32,2,128,128]{3,2,1,0:T(8,128)(2,1)} fusion(bf16[32,2,128,128]{3,2,1,0:T(8,128)(2,1)} %bitcast.65, pred[32,2]{1,0:T(8,128)(4,1)S(1)} %broadcast_in_dim.173), kind=kLoop, calls=%fused_computation.24 | loop fusion | flops 1048576 | bytes 4194368 | tf_op jit(solution)/shard_map/jit(_where)/select_n | solution.py:117
  20.1 0.3 select_reduce_fusion.4
  20.4 11.5 %all-to-all-start.1 = ((bf16[32,2,128,128]{3,2,1,0:T(8,128)(2,1)}), bf16[32,2,128,128]{3,2,1,0:T(8,128)(2,1)}, u32[]{:S(2)}, u32[]{:S(2)}) async-start(bf16[32,2,128,128]{3,2,1,0:T(8,128)(2,1)} %broadcast_select_fusion), calls=%async_computation.1 | async-start | bytes 4194304 | tf_op jit(solution)/shard_map/all_to_all | solution.py:119
  32.2 0.4 select_reduce_fusion.1
  33.0 0.3 select_reduce_fusion
  33.4 0.2 select_reduce_fusion.2
  34.0 47.0 %custom-call.9 = f32[64,8,8]{2,1,0:T(8,128)S(1)} custom-call(f32[64,8,8]{2,1,0:T(8,128)S(1)} %fusion.15), custom_call_target="Cholesky" | custom-call | tf_op jit(solution)/shard_map/jit(cholesky)/cholesky | solution.py:65
  81.2 3.7 %gather_fusion.1 = bf16[64,128,128]{2,1,0:T(8,128)(2,1)} fusion(bf16[64,128,128]{2,1,0:T(8,128)(2,1)} %bitcast.6, s32[1024]{0:T(1024)S(1)} %pad_clamp_fusion), kind=kCustom, calls=%fused_computation.1 | custom fusion | bytes 4194560 | tf_op jit(solution)/shard_map/gather | solution.py:131
  85.0 2.5 %fusion.11 = bf16[64,8,128]{2,1,0:T(8,128)(2,1)S(1)} fusion(bf16[64,128,128]{2,1,0:T(8,128)(2,1)} %gather_fusion.1, f32[8,128]{1,0:T(8,128)S(1)} %stack.2), kind=kOutput, calls=%fused_computation.27 | convolution fusion | flops 100728832 | bytes 2232320 | tf_op jit(solution)/shard_map/kp,cpl->ckl/dot_general | solution.py:144
  87.8 0.9 reshape.835
  88.6 8.6 %all-to-all-start.2 = ((bf16[16,2,2048]{2,1,0:T(2,128)(2,1)}), bf16[16,2,2048]{2,1,0:T(2,128)(2,1)S(1)}, u32[]{:S(2)}, u32[]{:S(2)}) async-start(bf16[16,2,2048]{2,1,0:T(2,128)(2,1)} %reshape.835), calls=%async_computation.2 | async-start | bytes 262144 | tf_op jit(solution)/shard_map/all_to_all | solution.py:24
  97.4 0.7 custom-call.10
  98.2 7.9 %all-to-all-done.2 = bf16[16,2,2048]{2,1,0:T(2,128)(2,1)S(1)} async-done(((bf16[16,2,2048]{2,1,0:T(2,128)(2,1)}), bf16[16,2,2048]{2,1,0:T(2,128)(2,1)S(1)}, u32[]{:S(2)}, u32[]{:S(2)}) %all-to-all-start.2) | async-done | bytes 131104 | tf_op jit(solution)/shard_map/all_to_all | solution.py:24
  106.6 0.7 fusion.35
  107.3 0.6 fusion.36
  108.0 1.1 reshape.837
  109.1 3.6 %all-to-all-start.3 = ((f32[16,1,4096]{2,1,0:T(1,128)}), f32[16,1,4096]{2,1,0:T(1,128)S(1)}, u32[]{:S(2)}, u32[]{:S(2)}) async-start(f32[16,1,4096]{2,1,0:T(1,128)} %reshape.837), calls=%async_computation.3 | async-start | bytes 524288 | tf_op jit(solution)/shard_map/all_to_all | solution.py:30
  113.0 4.1 %copy.70 = bf16[64,128,128]{1,2,0:T(8,128)(2,1)} copy(bf16[64,128,128]{2,1,0:T(8,128)(2,1)} %gather_fusion.1) | data formatting | bytes 4194304 | tf_op jit(solution)/shard_map/gather | solution.py:131
  117.1 6.8 %all-to-all-done.3 = f32[16,1,4096]{2,1,0:T(1,128)S(1)} async-done(((f32[16,1,4096]{2,1,0:T(1,128)}), f32[16,1,4096]{2,1,0:T(1,128)S(1)}, u32[]{:S(2)}, u32[]{:S(2)}) %all-to-all-start.3) | async-done | bytes 262176 | tf_op jit(solution)/shard_map/all_to_all | solution.py:30
  123.9 0.5 broadcast.876
  124.5 1.3 reduce.6
  125.7 0.2 reshape.838
  126.2 6.7 %convolution_bitcast_fusion = f32[64,128,128]{1,2,0:T(8,128)S(1)} fusion(f32[64,8,128]{2,1,0:T(8,128)S(1)} %copy.69, f32[8,128]{1,0:T(8,128)S(1)} %stack.2), kind=kOutput, calls=%fused_computation.23 | convolution fusion | flops 100663296 | bytes 4460544 | tf_op jit(solution)/shard_map/kp,ckl->cpl/dot_general | solution.py:149
  132.9 11.3 %fusion.10 = bf16[64,128,128]{1,2,0:T(8,128)(2,1)} fusion(f32[64,128,128]{1,2,0:T(8,128)S(1)} %convolution_bitcast_fusion, bf16[64,128,128]{1,2,0:T(8,128)(2,1)S(1)} %copy-done.1, f32[64,128]{1,0:T(8,128)S(1)} %get-tuple-element.32, f32[64,128]{1,0:T(8,128)S(1)} %get-tuple-element.31, f32[64,128]{1,0:T(8,128)S(1)} %get-tuple-element.30, ...), kind=kLoop, calls=%fused_computation.22 | loop fusion | flops 32505856 | bytes 8642560 | tf_op jit(solution)/shard_map/convert_element_type | solution.py:164
  144.2 4.1 %copy.71 = bf16[64,128,128]{2,1,0:T(8,128)(2,1)} copy(bf16[64,128,128]{1,2,0:T(8,128)(2,1)} %fusion.10) | data formatting | bytes 4194304 | tf_op jit(solution)/shard_map/convert_element_type | solution.py:164
  (69 shorter events, 3.9 us)
Async XLA Ops:
  0.0 14.8 %copy-start = (bf16[64,128,128]{2,1,0:T(8,128)(2,1)S(1)}, bf16[64,128,128]{2,1,0:T(8,128)(2,1)}, u32[]{:S(2)}) copy-start(bf16[64,128,128]{2,1,0:T(8,128)(2,1)} %param.8) | copy-start | bytes 6291460
  2.3 18.1 %all-to-all-start = ((f32[16,8,8]{2,1,0:T(8,128)}), f32[16,8,8]{2,1,0:T(8,128)S(1)}, u32[]{:S(2)}, u32[]{:S(2)}) async-start(f32[16,8,8]{2,1,0:T(8,128)} %broadcast_in_dim.172), calls=%async_computation | async-start | bytes 131072 | tf_op jit(solution)/shard_map/all_to_all | solution.py:30
  14.8 5.3 %copy-start.4 = (s32[2048]{0:T(1024)S(1)}, s32[2048]{0:T(1024)}, u32[]{:S(2)}) copy-start(s32[2048]{0:T(1024)} %param.9) | copy-start | bytes 24580
  14.8 5.3 %copy-start.5 = (s32[2048]{0:T(1024)S(1)}, s32[2048]{0:T(1024)}, u32[]{:S(2)}) copy-start(s32[2048]{0:T(1024)} %param.12) | copy-start | bytes 24580
  16.9 16.1 %copy-start.2 = (s32[2048,3]{0,1:T(4,128)S(1)}, s32[2048,3]{0,1:T(4,128)}, u32[]{:S(2)}) copy-start(s32[2048,3]{0,1:T(4,128)} %param.11) | copy-start | bytes 73732
  16.9 16.4 %copy-start.3 = (f32[2048]{0:T(1024)S(1)}, f32[2048]{0:T(1024)}, u32[]{:S(2)}) copy-start(f32[2048]{0:T(1024)} %param.13) | copy-start | bytes 24580
  20.4 60.8 %all-to-all-start.1 = ((bf16[32,2,128,128]{3,2,1,0:T(8,128)(2,1)}), bf16[32,2,128,128]{3,2,1,0:T(8,128)(2,1)}, u32[]{:S(2)}, u32[]{:S(2)}) async-start(bf16[32,2,128,128]{3,2,1,0:T(8,128)(2,1)} %broadcast_select_fusion), calls=%async_computation.1 | async-start | bytes 4194304 | tf_op jit(solution)/shard_map/all_to_all | solution.py:119
  88.6 17.5 %all-to-all-start.2 = ((bf16[16,2,2048]{2,1,0:T(2,128)(2,1)}), bf16[16,2,2048]{2,1,0:T(2,128)(2,1)S(1)}, u32[]{:S(2)}, u32[]{:S(2)}) async-start(bf16[16,2,2048]{2,1,0:T(2,128)(2,1)} %reshape.835), calls=%async_computation.2 | async-start | bytes 262144 | tf_op jit(solution)/shard_map/all_to_all | solution.py:24
  109.1 14.8 %all-to-all-start.3 = ((f32[16,1,4096]{2,1,0:T(1,128)}), f32[16,1,4096]{2,1,0:T(1,128)S(1)}, u32[]{:S(2)}, u32[]{:S(2)}) async-start(f32[16,1,4096]{2,1,0:T(1,128)} %reshape.837), calls=%async_computation.3 | async-start | bytes 524288 | tf_op jit(solution)/shard_map/all_to_all | solution.py:30
  126.2 6.7 %copy-start.1 = (bf16[64,128,128]{1,2,0:T(8,128)(2,1)S(1)}, bf16[64,128,128]{1,2,0:T(8,128)(2,1)}, u32[]{:S(2)}) copy-start(bf16[64,128,128]{1,2,0:T(8,128)(2,1)} %copy.70) | copy-start | bytes 6291460
where the time goes:
time: 149 us; the launch traced here: 148 us
  other arithmetic  69.6 us (47%)
  starting transfers between devices  33.8 us (23%)
  local copies, waits for them, and re-layouts  19.1 us (13%)
  waiting for transfers between devices  14.8 us (10%)
  matrix products  10.6 us (7%)
    another operation x4, other arithmetic, regress(): factor = jnp.linalg.cholesky(system)  47.1 us
    all_to_all x2, starting transfers between devices, sent_to_all(): lax.all_to_all(jnp.broadcast_to(shard[None], (size, *shard.shape)), axis,...  13.7 us
    all_to_all x1, starting transfers between devices, redistribute(): lax.all_to_all(outgoing, 'contract', split_axis=0, concat_axis=0, tiled=T...  11.5 us
    convert_element_type x1, other arithmetic, per_device(): result = values_now.astype(jnp.bfloat16)  11.3 us
    all_to_all x1, starting transfers between devices, summed_on_arrival(): lax.all_to_all(pieces, axis, split_axis=0, concat_axis=0, tiled=True)  8.61 us
    all_to_all x1, waiting for transfers between devices, summed_on_arrival(): lax.all_to_all(pieces, axis, split_axis=0, concat_axis=0, tiled=True)  7.94 us
    gather x2, local copies, waits for them, and re-layouts, redistribute(): incoming.reshape((block_count * capacity,) + grids.shape[1:])[chosen]  7.83 us
    all_to_all x2, waiting for transfers between devices, sent_to_all(): lax.all_to_all(jnp.broadcast_to(shard[None], (size, *shard.shape)), axis,...  6.84 us
  transfers between devices with their start and end apart: 4, of which 2 were waited for; matrix products, arithmetic and copies ran while one was open for 42% of the time, Pallas kernels for 0%

commit v1 on v0

v1 whole, which is shorter than its diff:
```python
import functools

import jax
import jax.numpy as jnp
from jax import lax
from jax.experimental import pallas as pl
from jax.experimental.pallas import tpu as pltpu
from jax.sharding import PartitionSpec as P

LEVELS = 128
BASIS = 8
OFFSETS = (-3, -2, -1, 1, 2, 3)
RIDGE = 0.05
DISCOUNT = 0.98
SPOT_SCALE = 0.25
Z, X = 8, 4
BLOCKS = Z * X
GROUP = 16
CON = 64
ROWS = len(OFFSETS) * 16
FIRST, SECOND = (4,), (3, 5, 2, 6, 1, 7, 0)
MESH = pl.DeviceIdType.MESH
MIB = 1024 * 1024


def order_kernel(position, order, places, count, sem):
    me = lax.axis_index("contract")
    copy = pltpu.make_async_copy(position, places, sem)
    copy.start()

    def clear(i, carry):
        count[i] = 0
        return carry

    lax.fori_loop(0, BLOCKS, clear, 0)
    copy.wait()

    def enter(i, carry):
        target = lax.shift_right_logical(places[me * CON + i], 6)
        rank = count[target]
        count[target] = rank + 1
        order[2 * target + rank] = i
        return carry

    lax.fori_loop(0, CON, enter, 0, unroll=4)


def split(value):
    high = value.astype(jnp.bfloat16)
    low = (value - high.astype(jnp.float32)).astype(jnp.bfloat16)
    return high, low


def place(block):
    return lax.rem(block, 2) * 16 + block // 2


def exchange_kernel(
    paths,
    prices_in,
    terminal_in,
    order_in,
    position_in,
    band_in,
    degree_in,
    actions_in,
    volume_in,
    arrived,
    gain,
    live,
    slots,
    prices,
    terminal,
    order,
    position,
    band,
    degree,
    actions,
    volume,
    sent,
    partial,
    slab,
    slab_in,
    row_out,
    row_in,
    share,
    moments,
    factor,
    table,
    left,
    params,
    ssem,
    rsem,
    fetch_sem,
):
    me = lax.axis_index("contract")
    mine = lax.axis_index("paths")
    z, x = me // X, lax.rem(me, X)

    def block(dz, dx):
        return lax.rem(z + dz + 2 * Z, Z) * X + lax.rem(x + dx + 2 * X, X)

    barrier = pltpu.get_barrier_semaphore()
    for dz in range(Z):
        for dx in range(X):
            if dz or dx:
                pl.semaphore_signal(barrier, inc=1, device_id=(mine, block(dz, dx)), device_id_type=MESH)
    for d in range(1, GROUP):
        pl.semaphore_signal(barrier, inc=1, device_id=(lax.rem(mine + d, GROUP), me), device_id_type=MESH)
    fetches = [
        pltpu.make_async_copy(src, dst, fetch_sem.at[n])
        for n, (src, dst) in enumerate(
            (
                (terminal_in, terminal),
                (order_in, order),
                (prices_in, prices),
                (position_in, position),
                (band_in, band),
                (degree_in, degree),
                (actions_in, actions),
                (volume_in, volume),
            )
        )
    ]
    for fetch in fetches:
        fetch.start()

    used = [0]
    started = []

    def send(src, dst, device):
        i = used[0]
        used[0] += 1
        copy = pltpu.make_async_remote_copy(
            src_ref=src, dst_ref=dst, send_sem=ssem.at[i], recv_sem=rsem.at[i],
            device_id=device, device_id_type=MESH,
        )
        copy.start()
        started.append(copy)
        return copy

    for fetch in fetches:
        fetch.wait()

    def arrange(i, carry):
        sent[i] = terminal[order[i]]
        return carry

    lax.fori_loop(0, CON, arrange, 0, unroll=2)

    price = prices[...]
    scaled = jnp.tanh(price)
    series = [jnp.ones_like(scaled), scaled]
    for _ in range(2, BASIS):
        series.append(2.0 * scaled * series[-1] - series[-2])
    spot = jnp.exp(SPOT_SCALE * price)
    basis = jnp.concatenate(series, axis=0)
    basis_high, basis_low = split(basis)
    both = jnp.concatenate([basis, spot, jnp.zeros((7, 128), jnp.float32)], axis=0)
    high, low = split(both)
    high, low = high.astype(jnp.float32), low.astype(jnp.float32)
    turned = jnp.transpose(jnp.concatenate([high, high, low, both, jnp.zeros((64, 128), jnp.float32)], axis=0))
    left[...] = turned[:, :48].astype(jnp.bfloat16)
    gram_part = lax.dot_general(
        basis, basis, (((1,), (1,)), ((), ())),
        precision=lax.Precision.HIGHEST, preferred_element_type=jnp.float32,
    )
    gram_part = jnp.concatenate([gram_part, jnp.zeros((BASIS, 120), jnp.float32)], axis=1)

    pl.semaphore_wait(barrier, BLOCKS - 1 + GROUP - 1)

    def pair(where):
        return pl.ds(2 * where, 2)

    grids = []

    def send_grids(shifts):
        for dz in shifts:
            for dx in range(X):
                if dz or dx:
                    to = block(dz, dx)
                    grids.append(send(sent.at[pair(to)], arrived.at[pair(place(me))], (mine, to)))

    send_grids(FIRST)

    basis_both = jnp.concatenate([basis_high, basis_low], axis=0)

    def one_target(t, carry):
        two = jnp.concatenate([sent[2 * t], sent[2 * t + 1]], axis=1)
        result = jnp.dot(basis_both, two, preferred_element_type=jnp.float32)
        result = result[:BASIS] + result[BASIS:]
        start = pl.multiple_of(16 * t, 16)
        partial[pl.ds(start, 8), :] = result[:, :128]
        partial[pl.ds(start + 8, 8), :] = result[:, 128:]
        return carry

    lax.fori_loop(0, BLOCKS, one_target, 0, unroll=4)
    for q in range(GROUP):
        slab[q, 0:32, :] = partial[pl.ds(q, 32, stride=16), :]
        slab[q, 32:40, :] = gram_part
    shares = []
    for d in range(1, GROUP):
        q = lax.rem(mine + d, GROUP)
        shares.append(send(slab.at[q], slab_in.at[mine], (q, me)))
    slab_in[mine] = slab[mine]
    table[...] = jnp.zeros_like(table)
    arrived[pair(place(me))] = sent[pair(me)]

    lane = lax.broadcasted_iota(jnp.int32, (16, 128), 1)
    lane_f = lane.astype(jnp.float32)
    places = position[...]
    low_bits = (places + lax.shift_left(band[...], 11) + lax.shift_left(degree[...], 19)).astype(jnp.float32)
    allowed = jnp.zeros((16, 128), jnp.int32)
    for a in range(3):
        moves = jnp.concatenate([actions[a : a + 1, 128 * row : 128 * row + 128] for row in range(16)], axis=0)
        for n, offset in enumerate(OFFSETS):
            allowed = jnp.bitwise_or(allowed, jnp.where(moves == offset, 1 << n, 0))
    high_bits = allowed.astype(jnp.float32)
    volumes = volume[...]
    target = lax.shift_right_logical(places, 6)
    for h in range(2):
        here = (target == me) & ((lane >= 64) if h else (lane < 64))
        first = jnp.min(jnp.where(here, lane_f, 1000.0), axis=1, keepdims=True)
        last = jnp.max(jnp.where(here, lane_f, -1.0), axis=1, keepdims=True)
        for r, index in enumerate((first, last)):
            chosen = lane_f == index
            for n, value in enumerate((low_bits, high_bits, volumes)):
                total = jnp.sum(jnp.where(chosen, value, 0.0), axis=1, keepdims=True)
                params[n, r, 16 * h : 16 * h + 16, :] = jnp.broadcast_to(total, (16, 128))
    lane32 = lax.broadcasted_iota(jnp.int32, (32, 128), 1)
    row32 = lax.broadcasted_iota(jnp.int32, (32, 128), 0)
    slot_row = jnp.zeros((1, 128), jnp.float32)
    for r in range(2):
        word = params[0, r].astype(jnp.int32)
        levels = jnp.bitwise_and(lax.shift_right_logical(word, 11), 255)
        live[r] = jnp.where(lane32 < levels, DISCOUNT, 0.0)
        slot = jnp.bitwise_and(word, 63).astype(jnp.float32)
        slot_row = slot_row + jnp.sum(jnp.where(lane32 == row32 + 32 * r, slot, 0.0), axis=0, keepdims=True)
    slots[...] = slot_row.astype(jnp.int32)

    for copy in shares:
        copy.wait_recv()
    total = slab_in[0]
    for q in range(1, GROUP):
        total = total + slab_in[q]
    row_out[...] = total[0:32].reshape(32, 1, 128)
    row_in[place(me)] = row_out[me]
    small = []
    for dz in range(Z):
        for dx in range(X):
            if dz or dx:
                to = block(dz, dx)
                small.append(send(row_out.at[to], row_in.at[place(me)], (mine, to)))
    send_grids(SECOND)

    eye = lax.broadcasted_iota(jnp.int32, (8, 128), 0) == lax.broadcasted_iota(jnp.int32, (8, 128), 1)
    system = total[32:40] / float(paths) + jnp.where(eye, RIDGE, 0.0)
    slot_of = {}
    for j in range(BASIS):
        inverse = 1.0 / jnp.sqrt(system[j : j + 1, j : j + 1])
        column = system[:, j : j + 1] * inverse
        across = system[j : j + 1, :] * inverse
        system = system - column * across
        slot_of[j, j] = len(slot_of)
        factor[slot_of[j, j]] = jnp.broadcast_to(inverse, (8, 128))
        for i in range(j + 1, BASIS):
            slot_of[i, j] = len(slot_of)
            factor[slot_of[i, j]] = jnp.broadcast_to(column[i : i + 1, :], (8, 128))

    for copy in small:
        copy.wait_recv()
    share[...] = row_in[...].reshape(32, 128)
    moments[mine] = share[...]
    gathers = []
    for d in range(1, GROUP):
        q = lax.rem(mine + d, GROUP)
        gathers.append(send(share, moments.at[mine], (q, me)))

    for copy in gathers:
        copy.wait_recv()
    lane8 = lax.broadcasted_iota(jnp.int32, (8, 128), 1)
    for tile in range(4):
        rows = slice(8 * tile, 8 * tile + 8)
        for r in range(2):
            word = params[0, r, rows, :].astype(jnp.int32)
            moves = params[1, r, rows, :].astype(jnp.int32)
            vol = params[2, r, rows, :]
            levels = jnp.bitwise_and(lax.shift_right_logical(word, 11), 255)
            highest = lax.shift_right_logical(word, 19)
            halfway, fitted = [], [None] * BASIS
            for i in range(BASIS):
                value = moments[8 * r + i, rows, :] / float(paths)
                for j in range(i):
                    value = value - factor[slot_of[i, j]] * halfway[j]
                halfway.append(value * factor[slot_of[i, i]])
            for i in reversed(range(BASIS)):
                value = halfway[i]
                for j in range(i + 1, BASIS):
                    value = value - factor[slot_of[j, i]] * fitted[j]
                fitted[i] = jnp.where(highest >= i, value * factor[slot_of[i, i]], 0.0)
            first = (16 * tile + r) * ROWS
            for n, offset in enumerate(OFFSETS):
                bit = jnp.bitwise_and(lax.shift_right_logical(moves, n), 1)
                to = lane8 + offset
                usable = (bit == 1) & (to >= 0) & (to < levels) & (lane8 < levels)
                for k in range(BASIS):
                    moved = pltpu.roll(fitted[k], (-offset) % LEVELS, 1)
                    table[pl.ds(first + 16 * n + k, 8, stride=2 * ROWS), :] = jnp.where(
                        usable, DISCOUNT * (moved - fitted[k]), 0.0
                    )
                table[pl.ds(first + 16 * n + BASIS, 8, stride=2 * ROWS), :] = jnp.where(
                    usable, -float(offset) * vol, 0.0
                )

    def best(c, carry):
        rows = table[pl.ds(pl.multiple_of(c * ROWS, 16), ROWS), :]
        value = jnp.zeros((128, 128), jnp.float32)
        for n in range(0, len(OFFSETS), 2):
            two = jnp.concatenate([rows[16 * n : 16 * n + 16], rows[16 * n + 16 : 16 * n + 32]], axis=1)
            two_high, two_low = split(two)
            right = jnp.concatenate([two_high, two_low, two_high], axis=0)
            result = jnp.dot(left[...], right, preferred_element_type=jnp.float32)
            value = jnp.maximum(value, jnp.maximum(result[:, :128], result[:, 128:]))
        gain[c] = value
        return carry

    lax.fori_loop(0, CON, best, 0, unroll=2)
    for copy in grids:
        copy.wait_recv()
    for copy in started:
        copy.wait_send()


SENDS = 2 * (BLOCKS - 1) + 2 * (GROUP - 1)


def finish_kernel(slots, arrived, gain, live, valued, ready, sem):
    for r in range(2):

        def one(row, carry):
            c = 2 * row + r
            kept = live[r, pl.ds(row, 1), :]
            ready[c] = (gain[c] + kept * arrived[c].astype(jnp.float32)).astype(jnp.bfloat16)
            pltpu.make_async_copy(ready.at[c], valued.at[slots[0, 32 * r + row]], sem).start()
            return carry

        lax.fori_loop(0, BLOCKS, one, 0)
    pltpu.make_async_copy(ready, valued, sem).wait()


def in_vmem(array):
    return pltpu.with_memory_space_constraint(array, pltpu.VMEM)


def kept_in_hbm(array):
    return pltpu.with_memory_space_constraint(array, pltpu.HBM)


def per_device(prices, terminal, band, position, actions, degree, volume):
    paths = prices.shape[1] * lax.axis_size("paths")
    con, width, levels = terminal.shape
    vmem = pl.BlockSpec(memory_space=pltpu.VMEM)
    anywhere = pl.BlockSpec(memory_space=pl.ANY)
    in_hbm = pl.BlockSpec(memory_space=pltpu.HBM)
    scalars = pl.BlockSpec(memory_space=pltpu.SMEM)
    grids = (con, width, levels)

    def table(array):
        return array.reshape(16, 128)

    order = pl.pallas_call(
        order_kernel,
        out_shape=jax.ShapeDtypeStruct((CON,), jnp.int32),
        in_specs=[in_hbm],
        out_specs=scalars,
        scratch_shapes=[
            pltpu.SMEM((CON * BLOCKS,), jnp.int32),
            pltpu.SMEM((BLOCKS,), jnp.int32),
            pltpu.SemaphoreType.DMA,
        ],
        compiler_params=pltpu.CompilerParams(vmem_limit_bytes=8 * MIB),
        name="order",
    )(kept_in_hbm(position))

    dma = pltpu.SemaphoreType.DMA
    f32, bf16 = jnp.float32, jnp.bfloat16
    arrived, gain, live, slots = pl.pallas_call(
        functools.partial(exchange_kernel, paths),
        out_shape=(
            pltpu.VMEM(grids, bf16),
            pltpu.VMEM(grids, f32),
            pltpu.VMEM((2, 32, 128), f32),
            jax.ShapeDtypeStruct((1, 128), jnp.int32),
        ),
        in_specs=[in_hbm] * 8,
        out_specs=(vmem,) * 4,
        scratch_shapes=[
            pltpu.VMEM((1, width), f32),
            pltpu.VMEM(grids, bf16),
            pltpu.SMEM((CON,), jnp.int32),
            pltpu.VMEM((16, 128), jnp.int32),
            pltpu.VMEM((16, 128), jnp.int32),
            pltpu.VMEM((16, 128), jnp.int32),
            pltpu.VMEM((3, 2048), jnp.int32),
            pltpu.VMEM((16, 128), f32),
            pltpu.VMEM(grids, bf16),
            pltpu.VMEM((512, 128), f32),
            pltpu.VMEM((GROUP, 40, 128), f32),
            pltpu.VMEM((GROUP, 40, 128), f32),
            pltpu.VMEM((32, 1, 128), f32),
            pltpu.VMEM((32, 1, 128), f32),
            pltpu.VMEM((32, 128), f32),
            pltpu.VMEM((GROUP, 32, 128), f32),
            pltpu.VMEM((36, 8, 128), f32),
            pltpu.VMEM((CON * ROWS, 128), f32),
            pltpu.VMEM((128, 48), bf16),
            pltpu.VMEM((3, 2, 32, 128), f32),
            dma((SENDS,)),
            dma((SENDS,)),
            dma((8,)),
        ],
        compiler_params=pltpu.CompilerParams(
            collective_id=0, has_side_effects=True, vmem_limit_bytes=24 * MIB
        ),
        name="exchange",
    )(
        *map(kept_in_hbm, (prices, terminal)),
        order,
        *map(kept_in_hbm, (*map(table, (position, band, degree)), actions.T, table(volume))),
    )

    return pl.pallas_call(
        finish_kernel,
        out_shape=jax.ShapeDtypeStruct(grids, bf16),
        in_specs=[scalars, vmem, vmem, vmem],
        out_specs=anywhere,
        scratch_shapes=[pltpu.VMEM(grids, bf16), dma],
        compiler_params=pltpu.CompilerParams(vmem_limit_bytes=16 * MIB),
        name="finish",
    )(slots, in_vmem(arrived), in_vmem(gain), in_vmem(live))


def solution(mesh):
    in_specs = (P(None, "paths"), P("contract", "paths", None), P(), P(), P(), P(), P())
    return jax.shard_map(
        per_device, mesh=mesh, in_specs=in_specs, out_specs=P("contract", "paths", None), check_vma=False
    )
```

time: 149 us -> 72.5 us (0.49)
  Pallas kernels: 0 us -> 72.3 us
  other arithmetic: 69.6 us -> 0 us
  starting transfers between devices: 33.8 us -> 0 us
  local copies, waits for them, and re-layouts: 19.1 us -> 0 us
  waiting for transfers between devices: 14.8 us -> 0 us
  matrix products: 10.6 us -> 0 us
    pallas_call x0 -> x3, Pallas kernels: none -> 72.3 us  [the longest x1 68.5 us: per_device(): pl.pallas_call(functools.partial(exchange_kernel, paths), out_shape=(pltp...]
    another operation x7 -> x0, other arithmetic: 47.8 us -> none  [the longest x4 47.1 us: regress(): factor = jnp.linalg.cholesky(system)]
    all_to_all x4 -> x0, starting transfers between devices: 33.8 us -> none  [the longest x2 13.7 us: sent_to_all(): lax.all_to_all(jnp.broadcast_to(shard[None], (size, *shard.shape)), axis,...]
    all_to_all x4 -> x0, waiting for transfers between devices: 14.8 us -> none  [the longest x1 7.94 us: summed_on_arrival(): lax.all_to_all(pieces, axis, split_axis=0, concat_axis=0, tiled=True)]
    convert_element_type x3 -> x0, other arithmetic: 11.4 us -> none  [the longest x1 11.3 us: per_device(): result = values_now.astype(jnp.bfloat16)]
    gather x3 -> x0, local copies, waits for them, and re-layouts: 9.97 us -> none  [the longest x2 7.83 us: redistribute(): incoming.reshape((block_count * capacity,) + grids.shape[1:])[chosen]]
    dot_general x3 -> x0, matrix products: 9.33 us -> none  [the longest x1 6.69 us: window(): estimate = jnp.einsum('kp,ckl->cpl', basis_rows, fitted, precision=highest)]
    convert_element_type x2 -> x0, local copies, waits for them, and re-layouts: 4.27 us -> none  [the longest x1 4.06 us: per_device(): result = values_now.astype(jnp.bfloat16)]
  transfers between devices with their start and end apart: 4 -> 0, of which waited for: 2 -> 0; matrix products, arithmetic and copies ran while one was open for 42% -> 0% of each run, Pallas kernels for 0% -> 0%
where the time goes in v1:
time: 72.5 us; the launch traced here: 72.3 us
  Pallas kernels  72.3 us (100%)
    pallas_call x1, Pallas kernels, per_device(): pl.pallas_call(functools.partial(exchange_kernel, paths), out_shape=(pltp...  68.5 us
    pallas_call x1, Pallas kernels, per_device(): pl.pallas_call(finish_kernel, out_shape=jax.ShapeDtypeStruct(grids, bf16)...  2.02 us
    pallas_call x1, Pallas kernels, per_device(): pl.pallas_call(order_kernel, out_shape=jax.ShapeDtypeStruct((CON,), jnp.i...  1.77 us

profile of v1, /device:TPU:1, one launch (start us, length us, event | category | flops | bytes accessed | tf_op | source)
XLA Modules:
  0.0 72.3 jit_solution(6192729215536792249)
XLA Ops:
  0.0 1.8 %order.1.order_in = s32[64]{0:T(128)S(1)} custom-call(s32[2048]{0:T(1024)} %position.1), custom_call_target="tpu_custom_call" | custom-call | tf_op jit(solution)/shard_map/order/pallas_call | solution.py:371
  1.8 68.5 %exchange.1 = (bf16[64,128,128]{2,1,0:T(8,128)(2,1)S(1)}, f32[64,128,128]{2,1,0:T(8,128)S(1)}, f32[2,32,128]{2,1,0:T(8,128)S(1)}, s32[1,128]{1,0:T(1,128)S(1)}) custom-call(f32[1,128]{1,0:T(1,128)} %prices_in.1, bf16[64,128,128]{2,1,0:T(8,128)(2,1)} %terminal_in.1, s32[64]{0:T(128)S(1)} %order.1.order_in, s32[16,128]{1,0:T(8,128)} %bitcast.6, ...), custom_call_target="tpu_custom_call" | custom-call | tf_op jit(solution)/shard_map/exchange/pallas_call | solution.py:387
  70.3 2.0 %finish.1 = bf16[64,128,128]{2,1,0:T(8,128)(2,1)} custom-call(s32[1,128]{1,0:T(1,128)S(1)} %get-tuple-element.9.slots, bf16[64,128,128]{2,1,0:T(8,128)(2,1)S(1)} %get-tuple-element.10.arrived, f32[64,128,128]{2,1,0:T(8,128)S(1)} %get-tuple-element.11.gain, f32[2,32,128]{2,1,0:T(8,128)S(1)} %get-tuple-element.12.live), custom_call_target="tpu_custom_call" | custom-call | tf_op jit(solution)/shard_map/finish/pallas_call | solution.py:432

commit v2 on v1

--- a/solution.py
+++ b/solution.py
@@ -18,31 +18,9 @@
 GROUP = 16
 CON = 64
 ROWS = len(OFFSETS) * 16
-FIRST, SECOND = (4,), (3, 5, 2, 6, 1, 7, 0)
+FIRST, SECOND, THIRD = (4,), (3, 5, 2), (6, 1, 7, 0)
 MESH = pl.DeviceIdType.MESH
 MIB = 1024 * 1024
-
-
-def order_kernel(position, order, places, count, sem):
-    me = lax.axis_index("contract")
-    copy = pltpu.make_async_copy(position, places, sem)
-    copy.start()
-
-    def clear(i, carry):
-        count[i] = 0
-        return carry
-
-    lax.fori_loop(0, BLOCKS, clear, 0)
-    copy.wait()
-
-    def enter(i, carry):
-        target = lax.shift_right_logical(places[me * CON + i], 6)
-        rank = count[target]
-        count[target] = rank + 1
-        order[2 * target + rank] = i
-        return carry
-
-    lax.fori_loop(0, CON, enter, 0, unroll=4)
 
 
 def split(value):
@@ -59,7 +37,6 @@
     paths,
     prices_in,
     terminal_in,
-    order_in,
     position_in,
     band_in,
     degree_in,
@@ -71,6 +48,7 @@
     slots,
     prices,
     terminal,
+    order_row,
     order,
     position,
     band,
@@ -82,6 +60,7 @@
     slab,
     slab_in,
     row_out,
+    row_mid,
     row_in,
     share,
     moments,
@@ -112,7 +91,6 @@
         for n, (src, dst) in enumerate(
             (
                 (terminal_in, terminal),
-                (order_in, order),
                 (prices_in, prices),
                 (position_in, position),
                 (band_in, band),
@@ -139,14 +117,19 @@
         started.append(copy)
         return copy
 
-    for fetch in fetches:
+    for fetch in fetches[1:]:
         fetch.wait()
-
-    def arrange(i, carry):
-        sent[i] = terminal[order[i]]
-        return carry
-
-    lax.fori_loop(0, CON, arrange, 0, unroll=2)
+    lane32 = lax.broadcasted_iota(jnp.int32, (32, 128), 1)
+    row32 = lax.broadcasted_iota(jnp.int32, (32, 128), 0)
+    half = lax.rem(me, 2) * 64
+    own = lax.shift_right_logical(position[pl.ds(me // 2, 1), :], 6)
+    going = (own == row32) & (lane32 >= half) & (lane32 < half + 64)
+    within = (lane32 - half).astype(jnp.float32)
+    first = jnp.min(jnp.where(going, within, 1000.0), axis=1, keepdims=True)
+    last = jnp.max(jnp.where(going, within, -1.0), axis=1, keepdims=True)
+    picked = jnp.where(lane32 == row32, first, 0.0) + jnp.where(lane32 == row32 + 32, last, 0.0)
+    picked = jnp.clip(jnp.sum(picked, axis=0, keepdims=True), 0.0, CON - 1.0)
+    order_row[...] = picked.astype(jnp.int32)
 
     price = prices[...]
     scaled = jnp.tanh(price)
@@ -156,6 +139,8 @@
     spot = jnp.exp(SPOT_SCALE * price)
     basis = jnp.concatenate(series, axis=0)
     basis_high, basis_low = split(basis)
+    ordered = pltpu.make_async_copy(order_row, order, fetch_sem.at[7])
+    ordered.start()
     both = jnp.concatenate([basis, spot, jnp.zeros((7, 128), jnp.float32)], axis=0)
     high, low = split(both)
     high, low = high.astype(jnp.float32), low.astype(jnp.float32)
@@ -166,6 +151,16 @@
         precision=lax.Precision.HIGHEST, preferred_element_type=jnp.float32,
     )
     gram_part = jnp.concatenate([gram_part, jnp.zeros((BASIS, 120), jnp.float32)], axis=1)
+
+    ordered.wait()
+    fetches[0].wait()
+
+    def arrange(t, carry):
+        sent[2 * t] = terminal[jnp.bitwise_and(order[0, t], CON - 1)]
+        sent[2 * t + 1] = terminal[jnp.bitwise_and(order[0, BLOCKS + t], CON - 1)]
+        return carry
+
+    lax.fori_loop(0, BLOCKS, arrange, 0)
 
     pl.semaphore_wait(barrier, BLOCKS - 1 + GROUP - 1)
 
@@ -227,8 +222,6 @@
             for n, value in enumerate((low_bits, high_bits, volumes)):
                 total = jnp.sum(jnp.where(chosen, value, 0.0), axis=1, keepdims=True)
                 params[n, r, 16 * h : 16 * h + 16, :] = jnp.broadcast_to(total, (16, 128))
-    lane32 = lax.broadcasted_iota(jnp.int32, (32, 128), 1)
-    row32 = lax.broadcasted_iota(jnp.int32, (32, 128), 0)
     slot_row = jnp.zeros((1, 128), jnp.float32)
     for r in range(2):
         word = params[0, r].astype(jnp.int32)
@@ -243,14 +236,12 @@
     total = slab_in[0]
     for q in range(1, GROUP):
         total = total + slab_in[q]
-    row_out[...] = total[0:32].reshape(32, 1, 128)
-    row_in[place(me)] = row_out[me]
-    small = []
-    for dz in range(Z):
-        for dx in range(X):
-            if dz or dx:
-                to = block(dz, dx)
-                small.append(send(row_out.at[to], row_in.at[place(me)], (mine, to)))
+    for zz in range(Z):
+        row_out[zz] = total[X * zz : X * zz + X].reshape(X, 1, 128)
+    row_mid[z] = row_out[z]
+    small_z = []
+    for dz in range(1, Z):
+        small_z.append(send(row_out.at[lax.rem(z + dz, Z)], row_mid.at[z], (mine, block(dz, 0))))
     send_grids(SECOND)
 
     eye = lax.broadcasted_iota(jnp.int32, (8, 128), 0) == lax.broadcasted_iota(jnp.int32, (8, 128), 1)
@@ -267,9 +258,17 @@
             slot_of[i, j] = len(slot_of)
             factor[slot_of[i, j]] = jnp.broadcast_to(column[i : i + 1, :], (8, 128))
 
-    for copy in small:
+    for copy in small_z:
         copy.wait_recv()
-    share[...] = row_in[...].reshape(32, 128)
+    row_in[x] = row_mid[:, x]
+    small_x = []
+    for dx in range(1, X):
+        small_x.append(send(row_mid.at[:, lax.rem(x + dx, X)], row_in.at[x], (mine, block(0, dx))))
+    send_grids(THIRD)
+    for copy in small_x:
+        copy.wait_recv()
+    for xx in range(X):
+        share[pl.ds(16 * (xx % 2) + xx // 2, Z, stride=2), :] = row_in[xx].reshape(Z, 128)
     moments[mine] = share[...]
     gathers = []
     for d in range(1, GROUP):
@@ -331,7 +330,7 @@
         copy.wait_send()
 
 
-SENDS = 2 * (BLOCKS - 1) + 2 * (GROUP - 1)
+SENDS = BLOCKS - 1 + Z - 1 + X - 1 + 2 * (GROUP - 1)
 
 
 def finish_kernel(slots, arrived, gain, live, valued, ready, sem):
@@ -367,20 +366,6 @@
 
     def table(array):
         return array.reshape(16, 128)
-
-    order = pl.pallas_call(
-        order_kernel,
-        out_shape=jax.ShapeDtypeStruct((CON,), jnp.int32),
-        in_specs=[in_hbm],
-        out_specs=scalars,
-        scratch_shapes=[
-            pltpu.SMEM((CON * BLOCKS,), jnp.int32),
-            pltpu.SMEM((BLOCKS,), jnp.int32),
-            pltpu.SemaphoreType.DMA,
-        ],
-        compiler_params=pltpu.CompilerParams(vmem_limit_bytes=8 * MIB),
-        name="order",
-    )(kept_in_hbm(position))
 
     dma = pltpu.SemaphoreType.DMA
     f32, bf16 = jnp.float32, jnp.bfloat16
@@ -392,12 +377,13 @@
             pltpu.VMEM((2, 32, 128), f32),
             jax.ShapeDtypeStruct((1, 128), jnp.int32),
         ),
-        in_specs=[in_hbm] * 8,
+        in_specs=[in_hbm] * 7,
         out_specs=(vmem,) * 4,
         scratch_shapes=[
             pltpu.VMEM((1, width), f32),
             pltpu.VMEM(grids, bf16),
-            pltpu.SMEM((CON,), jnp.int32),
+            pltpu.VMEM((1, 128), jnp.int32),
+            pltpu.SMEM((1, 128), jnp.int32),
             pltpu.VMEM((16, 128), jnp.int32),
             pltpu.VMEM((16, 128), jnp.int32),
             pltpu.VMEM((16, 128), jnp.int32),
@@ -407,8 +393,9 @@
             pltpu.VMEM((512, 128), f32),
             pltpu.VMEM((GROUP, 40, 128), f32),
             pltpu.VMEM((GROUP, 40, 128), f32),
-            pltpu.VMEM((32, 1, 128), f32),
-            pltpu.VMEM((32, 1, 128), f32),
+            pltpu.VMEM((Z, X, 1, 128), f32),
+            pltpu.VMEM((Z, X, 1, 128), f32),
+            pltpu.VMEM((X, Z, 1, 128), f32),
             pltpu.VMEM((32, 128), f32),
             pltpu.VMEM((GROUP, 32, 128), f32),
             pltpu.VMEM((36, 8, 128), f32),
@@ -425,7 +412,6 @@
         name="exchange",
     )(
         *map(kept_in_hbm, (prices, terminal)),
-        order,
         *map(kept_in_hbm, (*map(table, (position, band, degree)), actions.T, table(volume))),
     )
 

time: 72.5 us -> 70.1 us (0.967)
  Pallas kernels: 72.3 us -> 70 us
    pallas_call x1 -> x0, Pallas kernels: 1.77 us -> none  [per_device(): pl.pallas_call(order_kernel, out_shape=jax.ShapeDtypeStruct((CON,), jnp.i...]
where the time goes in v2:
time: 70.1 us; the launch traced here: 70 us
  Pallas kernels  70 us (100%)
    pallas_call x1, Pallas kernels, per_device(): pl.pallas_call(functools.partial(exchange_kernel, paths), out_shape=(pltp...  67.9 us
    pallas_call x1, Pallas kernels, per_device(): pl.pallas_call(finish_kernel, out_shape=jax.ShapeDtypeStruct(grids, bf16)...  2.02 us

profile of v2, /device:TPU:1, one launch (start us, length us, event | category | flops | bytes accessed | tf_op | source)
XLA Modules:
  0.0 70.0 jit_solution(2616204880553047049)
XLA Ops:
  0.0 67.9 %exchange.1 = (bf16[64,128,128]{2,1,0:T(8,128)(2,1)S(1)}, f32[64,128,128]{2,1,0:T(8,128)S(1)}, f32[2,32,128]{2,1,0:T(8,128)S(1)}, s32[1,128]{1,0:T(1,128)S(1)}) custom-call(f32[1,128]{1,0:T(1,128)} %prices_in.1, bf16[64,128,128]{2,1,0:T(8,128)(2,1)} %terminal_in.1, s32[16,128]{1,0:T(8,128)} %bitcast.6, s32[16,128]{1,0:T(8,128)} %bitcast.7, ...), custom_call_target="tpu_custom_call" | custom-call | tf_op jit(solution)/shard_map/exchange/pallas_call | solution.py:372
  67.9 2.0 %finish.1 = bf16[64,128,128]{2,1,0:T(8,128)(2,1)} custom-call(s32[1,128]{1,0:T(1,128)S(1)} %get-tuple-element.9.slots, bf16[64,128,128]{2,1,0:T(8,128)(2,1)S(1)} %get-tuple-element.10.arrived, f32[64,128,128]{2,1,0:T(8,128)S(1)} %get-tuple-element.11.gain, f32[2,32,128]{2,1,0:T(8,128)S(1)} %get-tuple-element.12.live), custom_call_target="tpu_custom_call" | custom-call | tf_op jit(solution)/shard_map/finish/pallas_call | solution.py:418

commit v3 on v2

--- a/solution.py
+++ b/solution.py
@@ -18,7 +18,7 @@
 GROUP = 16
 CON = 64
 ROWS = len(OFFSETS) * 16
-FIRST, SECOND, THIRD = (4,), (3, 5, 2), (6, 1, 7, 0)
+FIRST, SECOND, THIRD = (4, 0), (3, 5, 2), (6, 1, 7)
 MESH = pl.DeviceIdType.MESH
 MIB = 1024 * 1024
 
@@ -170,8 +170,8 @@
     grids = []
 
     def send_grids(shifts):
-        for dz in shifts:
-            for dx in range(X):
+        for dx in (2, 1, 3, 0):
+            for dz in shifts:
                 if dz or dx:
                     to = block(dz, dx)
                     grids.append(send(sent.at[pair(to)], arrived.at[pair(place(me))], (mine, to)))

time: 70.1 us -> 67.7 us (0.966)
  Pallas kernels: 70 us -> 67.6 us
    pallas_call x1, Pallas kernels: 67.9 us -> 65.6 us  [per_device(): pl.pallas_call(functools.partial(exchange_kernel, paths), out_shape=(pltp...]
where the time goes in v3:
time: 67.7 us; the launch traced here: 67.6 us
  Pallas kernels  67.6 us (100%)
    pallas_call x1, Pallas kernels, per_device(): pl.pallas_call(functools.partial(exchange_kernel, paths), out_shape=(pltp...  65.6 us
    pallas_call x1, Pallas kernels, per_device(): pl.pallas_call(finish_kernel, out_shape=jax.ShapeDtypeStruct(grids, bf16)...  2.02 us

profile of v3, /device:TPU:1, one launch (start us, length us, event | category | flops | bytes accessed | tf_op | source)
XLA Modules:
  0.0 67.6 jit_solution(2528267438812879304)
XLA Ops:
  0.0 65.6 %exchange.1 = (bf16[64,128,128]{2,1,0:T(8,128)(2,1)S(1)}, f32[64,128,128]{2,1,0:T(8,128)S(1)}, f32[2,32,128]{2,1,0:T(8,128)S(1)}, s32[1,128]{1,0:T(1,128)S(1)}) custom-call(f32[1,128]{1,0:T(1,128)} %prices_in.1, bf16[64,128,128]{2,1,0:T(8,128)(2,1)} %terminal_in.1, s32[16,128]{1,0:T(8,128)} %bitcast.6, s32[16,128]{1,0:T(8,128)} %bitcast.7, ...), custom_call_target="tpu_custom_call" | custom-call | tf_op jit(solution)/shard_map/exchange/pallas_call | solution.py:372
  65.6 2.0 %finish.1 = bf16[64,128,128]{2,1,0:T(8,128)(2,1)} custom-call(s32[1,128]{1,0:T(1,128)S(1)} %get-tuple-element.9.slots, bf16[64,128,128]{2,1,0:T(8,128)(2,1)S(1)} %get-tuple-element.10.arrived, f32[64,128,128]{2,1,0:T(8,128)S(1)} %get-tuple-element.11.gain, f32[2,32,128]{2,1,0:T(8,128)S(1)} %get-tuple-element.12.live), custom_call_target="tpu_custom_call" | custom-call | tf_op jit(solution)/shard_map/finish/pallas_call | solution.py:418
